TPU v7x, 128 devices: a whole 4x4x4 slice. The times are simulated.
128 devices in a mesh: rows: 16 (over x, z_lo, core), planes: 8 (over y, z_hi).
Axes of the slice: x: 4, y: 4, z: 4 (z_hi: 2, z_lo: 2; z = z_hi * 2 + z_lo), core: 2. Of those that a mesh axis runs over, the one named last changes fastest.
Arguments:
- density: float32 [8, 4096, 4096], P('planes', 'rows'), may hold values from -6 to 6
- lens_weight: float32 [8], P('planes'), may hold values from 0.05 to 0.5
- spectrum_bin: int32 [4096, 4096], P(None, ('rows', 'planes')), may hold values from 0 to 63, as said below
Outputs:
- shear_real: float32 [4096, 4096], P(('rows', 'planes'))
- shear_imag: float32 [4096, 4096], P(('rows', 'planes'))
- spectrum: float32 [64], replicated
Inputs may be any that keep to these rules, and one draw needn't show every extreme that they name: `spectrum_bin`: each Fourier pixel's band.
All inputs are finite; a program needn't handle non-finite values.
Results may differ from a plain program's by a relative error of at most 0.0003.
Values sent between devices are 32-bit elements; how exact they have to be, the bound alone decides.
A program may use at most 64 MiB of HBM per device.

v0:
```python
from functools import partial
import math

import jax
import jax.numpy as jnp
import ml_dtypes
import numpy as np
from jax import lax
from jax.experimental import pallas as pl
from jax.experimental.pallas import tpu as pltpu
from jax.sharding import Mesh
from jax.sharding import PartitionSpec as P

N = 4096
NBINS = 64
DEVICES = 128
AXES = ("x", "zl", "core", "y", "zh")
ROWS = ("x", "zl", "core")
PLANES = ("y", "zh")
LOGICAL = pl.DeviceIdType.LOGICAL
F32 = jnp.float32
BF16 = jnp.bfloat16


def halves(table):
    high = table.astype(np.float32).astype(ml_dtypes.bfloat16)
    low = (table - high.astype(np.float64)).astype(np.float32).astype(ml_dtypes.bfloat16)
    return np.stack([high, low])


def make_tables():
    turn = 2.0 * math.pi
    i128 = np.arange(128)
    angle = turn * ((i128[:, None] * i128[None, :]) % 128) / 128
    cos, sin = np.cos(angle), np.sin(angle)
    forward = np.block([[cos, sin], [-sin, cos]])
    inverse = np.block([[cos, -sin], [sin, cos]])
    first = np.zeros((256, 256))
    back = np.zeros((256, 256))
    for d in range(128):
        if d < 64:
            phase = turn * (((16 + 32 * d) * i128) % 4096) / 4096
            first[d, 128:] = np.cos(phase)
            first[128 + d, 128:] = -np.sin(phase)
            weight = 2.0
        elif d == 64:
            first[d, :128] = 1.0
            first[128 + d, :128] = (-1.0) ** i128
            weight = 1.0
        else:
            phase = turn * ((d * i128) % 128) / 128
            first[d, :128] = np.cos(phase)
            first[128 + d, :128] = -np.sin(phase)
            weight = 2.0
        back[:, d] = weight * first[d]
        back[:, 128 + d] = weight * first[128 + d]
    small = np.zeros((4, 32, 32, 4), np.complex128)
    i32 = np.arange(32)
    kernel = np.exp(-1j * turn * ((i32[:, None] * i32[None, :]) % 32) / 32)
    for c in range(4):
        small[c, :, :, c] = kernel
    small = small.reshape(128, 128)
    lanes = np.block([[small.real, small.imag], [-small.imag, small.real]])
    wide = np.conj(small).T
    lanes_back = np.block([[wide.real, wide.imag], [-wide.imag, wide.real]])
    mats = np.stack([halves(t) for t in (forward, inverse, first, back, lanes, lanes_back)])
    y2 = np.tile(i32, 4)
    phase = turn * (i128[:, None] * y2[None, :]) / 4096
    column_twiddle = np.stack([np.cos(phase), np.sin(phase)]).astype(np.float32)
    phase = turn * (np.arange(16)[:, None] * i128[None, :]) / 4096
    row_twiddle = np.stack([np.cos(phase), np.sin(phase)]).astype(np.float32)
    return mats, column_twiddle, row_twiddle


FORWARD, INVERSE, FIRST, BACK, LANES, LANES_BACK = range(6)


def rfft(values):
    n = len(values)
    if n == 2:
        return [(values[0] + values[1], None), (values[0] - values[1], None)]
    even, odd = rfft(values[0::2]), rfft(values[1::2])
    out = [None] * (n // 2 + 1)
    out[0] = (even[0][0] + odd[0][0], None)
    out[n // 2] = (even[0][0] - odd[0][0], None)
    for k in range(1, n // 4):
        c, s = math.cos(2 * math.pi * k / n), math.sin(2 * math.pi * k / n)
        er, ei = even[k]
        orr, oi = odd[k]
        if 8 * k == n:
            pr, pi = (orr + oi) * c, (oi - orr) * c
        else:
            pr, pi = orr * c + oi * s, oi * c - orr * s
        out[k] = (er + pr, ei + pi)
        out[n // 2 - k] = (er - pr, pi - ei)
    out[n // 4] = (even[n // 4][0], -odd[n // 4][0])
    return out


def irfft(g):
    n = 2 * (len(g) - 1)
    if n == 2:
        return [g[0][0] + g[1][0], g[0][0] - g[1][0]]
    even, odd = [None] * (n // 4 + 1), [None] * (n // 4 + 1)
    even[0] = (g[0][0] + g[n // 2][0], None)
    odd[0] = (g[0][0] - g[n // 2][0], None)
    for k in range(1, n // 4):
        c, s = math.cos(2 * math.pi * k / n), math.sin(2 * math.pi * k / n)
        ar, ai = g[k]
        br, bi = g[n // 2 - k]
        even[k] = (ar + br, ai - bi)
        dr, di = ar - br, ai + bi
        odd[k] = (dr * c - di * s, dr * s + di * c)
    mr, mi = g[n // 4]
    even[n // 4] = (mr + mr, None)
    odd[n // 4] = (-(mi + mi), None)
    a, b = irfft(even), irfft(odd)
    out = [None] * n
    out[0::2], out[1::2] = a, b
    return out


def split(value):
    high = value.astype(BF16)
    return high, (value - high.astype(F32)).astype(BF16)


def table_times(mats, which, data):
    high, low = split(data)
    dot = partial(jnp.dot, preferred_element_type=F32)
    return dot(mats[which, 0], high) + dot(mats[which, 0], low) + dot(mats[which, 1], high)


def times_table(mats, which, data):
    high, low = split(data)
    dot = partial(jnp.dot, preferred_element_type=F32)
    return dot(high, mats[which, 0]) + dot(low, mats[which, 0]) + dot(high, mats[which, 1])


def my_index():
    x, zl, core, y, zh = (lax.axis_index(a) for a in AXES)
    return ((x * 2 + zl) * 2 + core) * 8 + y * 2 + zh


def row_forward(res, mats, rtw, ubuf, msg):
    for q in range(4):
        rows = pl.ds(q * 8, 8)
        out = rfft([res[rows, pl.ds(x1 * 128, 128)] for x1 in range(32)])
        for k1 in range(16):
            at = pl.ds(k1 * 32 + q * 8, 8)
            if k1 == 0:
                ubuf[0, at, :], ubuf[1, at, :] = out[0][0], out[16][0]
            else:
                tr, ti = rtw[0, pl.ds(k1, 1), :], rtw[1, pl.ds(k1, 1), :]
                ur, ui = out[k1]
                ubuf[0, at, :] = ur * tr + ui * ti
                ubuf[1, at, :] = ui * tr - ur * ti
    data = jnp.concatenate([ubuf[0].T, ubuf[1].T], axis=0)
    spread = table_times(mats, FORWARD, data)
    special = table_times(mats, FIRST, data[:, :128])
    lane = lax.broadcasted_iota(jnp.int32, (256, 128), 1)
    for t in range(4):
        piece = spread[:, t * 128 : (t + 1) * 128]
        if t == 0:
            piece = jnp.where(lane < 32, special, piece)
        for c in range(2):
            msg[pl.ds(c * 4 + t, 128, stride=8), :] = piece[c * 128 : (c + 1) * 128]


def column_part(me, recv, mats, ctw, power, msg):
    lane = lax.broadcasted_iota(jnp.int32, (128, 128), 1)
    sub = lax.broadcasted_iota(jnp.int32, (128, 128), 0)
    special = jnp.logical_and(lane < 32, me == 64)
    re = [recv[pl.ds(t, 128, stride=8), :] for t in range(4)]
    im = [recv[pl.ds(4 + t, 128, stride=8), :] for t in range(4)]
    zero = jnp.zeros((128, 128), F32)
    re.append(jnp.where(special, im[0], zero))
    im[0] = jnp.where(special, zero, im[0])
    im.append(zero)
    data = jnp.concatenate([jnp.concatenate(re, axis=1), jnp.concatenate(im, axis=1)], axis=0)
    y = table_times(mats, FORWARD, data)
    tc, ts = ctw[0], ctw[1]
    rows = []
    for t in range(5):
        yr, yi = y[:128, t * 128 : (t + 1) * 128], y[128:, t * 128 : (t + 1) * 128]
        rows.append(jnp.concatenate([yr * tc + yi * ts, yi * tc - yr * ts], axis=1))
    f = times_table(mats, LANES, jnp.concatenate(rows, axis=0))
    ky2 = lane // 4
    col = lane % 4
    ky = sub + 128 * ky2
    nyquist = ky == 2048
    ky = jnp.where(ky >= 2048, ky - 4096, ky).astype(F32)
    scale = 1.0 / (float(N) * float(N))
    hats = []
    for t in range(5):
        fr, fi = f[t * 128 : (t + 1) * 128, :128], f[t * 128 : (t + 1) * 128, 128:]
        if t < 4:
            slot = t * 4 + col
            kx = slot + 32 * me
            if t == 0:
                zeroth = jnp.where(
                    me < 64, 16 + 32 * me, jnp.where(me == 64, 0, 32 * me)
                )
                kx = jnp.where(slot == 0, zeroth, kx)
            kx = jnp.where(kx >= 2048, kx - 4096, kx).astype(F32)
        else:
            kx = jnp.full((128, 128), -2048.0, F32)
        norm = kx * kx + ky * ky
        if t == 0:
            anchor = norm == 0
            norm = jnp.where(anchor, 1.0, norm)
            fr, fi = jnp.where(anchor, 0.0, fr), jnp.where(anchor, 0.0, fi)
        power[t] = fr * fr + fi * fi
        inv = scale / norm
        kr = (kx * kx - ky * ky) * inv
        ki = 2.0 * kx * ky * inv
        if t < 4:
            kn = jnp.where(nyquist, ki, 0.0)
            ki = jnp.where(nyquist, 0.0, ki)
            a = (kr * fr - kn * fi, kr * fi + kn * fr)
            c = (ki * fr, ki * fi)
        else:
            kn = jnp.where(nyquist, ki, 0.0)
            ki = jnp.where(nyquist, 0.0, ki)
            a = (kr * fr - ki * fi, kr * fi + ki * fr)
            c = (kn * fr, kn * fi)
        hats.append((a, c))
    rows = [jnp.concatenate(hats[t][ac], axis=1) for ac in range(2) for t in range(5)]
    g = times_table(mats, LANES_BACK, jnp.concatenate(rows, axis=0))
    re, im = [], []
    for i in range(10):
        gr, gi = g[i * 128 : (i + 1) * 128, :128], g[i * 128 : (i + 1) * 128, 128:]
        re.append(gr * tc - gi * ts)
        im.append(gi * tc + gr * ts)
    data = jnp.concatenate([jnp.concatenate(re, axis=1), jnp.concatenate(im, axis=1)], axis=0)
    s = table_times(mats, INVERSE, data)
    for ac in range(2):
        for t in range(4):
            at = (ac * 5 + t) * 128
            sr, si = s[:128, at : at + 128], s[128:, at : at + 128]
            if t == 0:
                extra = (ac * 5 + 4) * 128
                si = jnp.where(special, s[:128, extra : extra + 128], si)
            msg[pl.ds(ac * 8 + t, 128, stride=16), :] = sr
            msg[pl.ds(ac * 8 + 4 + t, 128, stride=16), :] = si


def row_inverse(recv, mats, rtw, vbuf, outs):
    lane = lax.broadcasted_iota(jnp.int32, (256, 128), 1)
    for ac in range(2):
        parts = [
            jnp.concatenate(
                [recv[pl.ds(ac * 8 + c * 4 + t, 128, stride=16), :] for t in range(4)], axis=1
            )
            for c in range(2)
        ]
        data = jnp.concatenate(parts, axis=0)
        v = table_times(mats, INVERSE, data)
        special = table_times(mats, BACK, data[:, :128])
        first = jnp.where(lane < 32, special, v[:, :128])
        for c in range(2):
            rows = slice(c * 128, (c + 1) * 128)
            full = jnp.concatenate([first[rows], v[rows, 128:]], axis=1)
            vbuf[c] = full.T
        for q in range(4):
            g = [None] * 17
            for k1 in range(16):
                at = pl.ds(k1 * 32 + q * 8, 8)
                vr, vi = vbuf[0, at, :], vbuf[1, at, :]
                if k1 == 0:
                    g[0], g[16] = (vr, None), (vi, None)
                else:
                    tr, ti = rtw[0, pl.ds(k1, 1), :], rtw[1, pl.ds(k1, 1), :]
                    g[k1] = (vr * tr - vi * ti, vi * tr + vr * ti)
            out = irfft(g)
            for x1 in range(32):
                outs[ac][pl.ds(q * 8, 8), pl.ds(x1 * 128, 128)] = out[x1]


def send_all(me, msg, recv, send, arrive, rows):
    def step(i, _):
        to = lax.rem(me + i, DEVICES)
        pltpu.make_async_remote_copy(
            src_ref=msg.at[pl.ds(pl.multiple_of(to * rows, rows), rows)],
            dst_ref=recv.at[pl.ds(pl.multiple_of(me * rows, rows), rows)],
            send_sem=send,
            recv_sem=arrive,
            device_id=to,
            device_id_type=LOGICAL,
        ).start()
        return 0

    lax.fori_loop(1, DEVICES, step, 0)
    own = pl.ds(pl.multiple_of(me * rows, rows), rows)
    recv[own, :] = msg[own, :]


def wait_all(buf, sem, rows):
    part = buf.at[pl.ds(0, (DEVICES - 1) * rows)]
    pltpu.make_async_copy(part, part, sem).wait()


def bin_power(bins, power, acc, spec):
    def group(g, _):
        sums = [jnp.zeros((8, 128), F32) for _ in range(8)]
        for i in range(9):
            t = i % 5 if i < 5 else i - 5
            which = 0 if i < 5 else 1
            for r in range(16):
                at = pl.ds(r * 8, 8)
                b = bins[which, t, at, :] - g * 8
                p = power[t, at, :]
                for k in range(8):
                    sums[k] = sums[k] + jnp.where(b == k, p, 0.0)
        rows = [jnp.sum(v, axis=0, keepdims=True) for v in sums]
        acc[pl.ds(pl.multiple_of(g * 8, 8), 8), :] = jnp.concatenate(rows, axis=0)
        return 0

    lax.fori_loop(0, 8, group, 0)
    acc[pl.ds(64, 64), :] = jnp.zeros((64, 128), F32)
    row = jnp.sum(acc[...].T, axis=0, keepdims=True)
    spec[0] = row * (NBINS / float(N) ** 4)


def reduce_planes(weight, mine, res, yf, zf, yrelay, ydirect, yfinal, zrecv, zsum, ssem, rsem):
    y, zh = lax.axis_index("y"), lax.axis_index("zh")
    base = my_index() - y * 2 - zh
    up, down, across = lax.rem(y + 1, 4), lax.rem(y + 3, 4), lax.rem(y + 2, 4)
    dev_up, dev_down = base + up * 2 + zh, base + down * 2 + zh
    dev_z = base + y * 2 + (1 - zh)
    count = [0]
    sends = []

    def send(src, dst, to):
        i = count[0]
        count[0] += 1
        copy = pltpu.make_async_remote_copy(
            src_ref=src,
            dst_ref=dst,
            send_sem=ssem.at[i],
            recv_sem=rsem.at[i],
            device_id=to,
            device_id_type=LOGICAL,
        )
        copy.start()
        sends.append(copy)
        return copy

    def share(t, h, q):
        return mine.at[pl.ds(pl.multiple_of((t * 2 + h) * 32 + q * 8, 8), 8)]

    znew = {}
    for q in zf:
        for i, t in enumerate((across, up, down, y)):
            znew[q, i] = send(share(t, 1 - zh, q), zrecv.at[q, i], dev_z)
    relay, direct, final = {}, {}, {}
    for q in yf:
        relay[q, 0] = send(share(across, 0, q), yrelay.at[q, 0], dev_up)
        relay[q, 1] = send(share(across, 1, q), yrelay.at[q, 1], dev_down)
        direct[q, 0] = send(share(up, 1, q), ydirect.at[q, 1], dev_up)
        direct[q, 1] = send(share(down, 0, q), ydirect.at[q, 0], dev_down)
    half = (slice(0, 2048), slice(2048, 4096))

    def y_relay_first(q):
        relay[q, 0].wait_recv()
        yrelay[q, 0] = yrelay[q, 0] + share(up, 0, q)[...]
        final[q, 0] = send(yrelay.at[q, 0], yfinal.at[q, 0], dev_up)
        relay[q, 1].wait_recv()
        yrelay[q, 1] = yrelay[q, 1] + share(down, 1, q)[...]
        final[q, 1] = send(yrelay.at[q, 1], yfinal.at[q, 1], dev_down)

    def y_finish_first(q):
        for h in range(2):
            direct[q, h].wait_recv()
            final[q, h].wait_recv()
        for h in range(2):
            yfinal[q, h] = yfinal[q, h] + ydirect[q, h] + share(y, h, q)[...]
        znew[q, 0] = send(yfinal.at[q, 1 - zh], zrecv.at[q, 0], dev_z)

    def z_last(q):
        znew[q, 0].wait_recv()
        res[pl.ds(q * 8, 8), :] = zrecv[q, 0] + yfinal[q, zh]

    def z_first(q):
        for i, t in enumerate((across, up, down, y)):
            znew[q, i].wait_recv()
            zsum[q, i] = zrecv[q, i] + share(t, zh, q)[...]
            if i == 0:
                relay[q, 0] = send(
                    zsum.at[q, 0, :, pl.ds(0, 2048)], yrelay.at[q, 0, :, pl.ds(0, 2048)], dev_up
                )
                relay[q, 1] = send(
                    zsum.at[q, 0, :, pl.ds(2048, 2048)], yrelay.at[q, 1, :, pl.ds(0, 2048)], dev_down
                )
            if i == 1:
                direct[q, 0] = send(
                    zsum.at[q, 1, :, pl.ds(2048, 2048)], ydirect.at[q, 1, :, pl.ds(0, 2048)], dev_up
                )
            if i == 2:
                direct[q, 1] = send(
                    zsum.at[q, 2, :, pl.ds(0, 2048)], ydirect.at[q, 0, :, pl.ds(0, 2048)], dev_down
                )

    def y_relay_last(q):
        relay[q, 0].wait_recv()
        yrelay[q, 0, :, :2048] = yrelay[q, 0, :, :2048] + zsum[q, 1, :, half[0]]
        final[q, 0] = send(
            yrelay.at[q, 0, :, pl.ds(0, 2048)], yfinal.at[q, 0, :, pl.ds(0, 2048)], dev_up
        )
        relay[q, 1].wait_recv()
        yrelay[q, 1, :, :2048] = yrelay[q, 1, :, :2048] + zsum[q, 2, :, half[1]]
        final[q, 1] = send(
            yrelay.at[q, 1, :, pl.ds(0, 2048)], yfinal.at[q, 1, :, pl.ds(0, 2048)], dev_down
        )

    def y_last(q):
        for h in range(2):
            direct[q, h].wait_recv()
            final[q, h].wait_recv()
        for h in range(2):
            res[pl.ds(q * 8, 8), half[h]] = (
                zsum[q, 3, :, half[h]] + yfinal[q, h, :, :2048] + ydirect[q, h, :, :2048]
            )

    y_relay_first(yf[0])
    y_relay_first(yf[1])
    y_finish_first(yf[0])
    z_first(zf[0])
    y_relay_last(zf[0])
    y_finish_first(yf[1])
    z_first(zf[1])
    y_relay_last(zf[1])
    y_last(zf[0])
    z_last(yf[0])
    z_last(yf[1])
    y_last(zf[1])
    return sends


def kernel(
    density, weight, bins, mats_in, ctw, rtw, out_real, out_imag, out_spec,
    mine, res, mats, yrelay, ydirect, yfinal, zrecv, zsum,
    ubuf, msgb, recvb, msgc, recvc, power, acc, spec, specs,
    lsem, msem, ssem, rsem, asem,
):
    me = my_index()
    barrier = pltpu.get_barrier_semaphore()
    loads = []
    for i in range(8):
        copy = pltpu.make_async_copy(
            density.at[0, pl.ds(i * 32, 32)], mine.at[pl.ds(i * 32, 32)], lsem.at[i]
        )
        copy.start()
        loads.append(copy)
    mload = pltpu.make_async_copy(mats_in, mats, msem)
    mload.start()

    def greet(i, _):
        pl.semaphore_signal(
            barrier, inc=1, device_id=lax.rem(me + i, DEVICES), device_id_type=LOGICAL
        )
        return 0

    lax.fori_loop(1, DEVICES, greet, 0)
    w = weight[0]
    for i in range(8):
        loads[i].wait()
        rows = pl.ds(i * 32, 32)
        mine[rows, :] = mine[rows, :] * w
    pl.semaphore_wait(barrier, DEVICES - 1)
    sends = reduce_planes(
        weight, mine, res, (0, 1), (2, 3), yrelay, ydirect, yfinal, zrecv, zsum, ssem, rsem
    )
    mload.wait()
    row_forward(res, mats, rtw, ubuf, msgb)
    send_all(me, msgb, recvb, asem.at[0], asem.at[1], 8)
    wait_all(recvb, asem.at[1], 8)
    column_part(me, recvb, mats, ctw, power, msgc)
    send_all(me, msgc, recvc, asem.at[2], asem.at[3], 16)
    bin_power(bins, power, acc, spec)

    def share_spec(i, _):
        to = lax.rem(me + i, DEVICES)
        pltpu.make_async_remote_copy(
            src_ref=spec.at[0],
            dst_ref=specs.at[me],
            send_sem=asem.at[4],
            recv_sem=asem.at[5],
            device_id=to,
            device_id_type=LOGICAL,
        ).start()
        return 0

    lax.fori_loop(1, DEVICES, share_spec, 0)
    specs[me] = spec[0]
    wait_all(recvc, asem.at[3], 16)
    row_inverse(recvc, mats, rtw, ubuf, (out_real, out_imag))
    wait_all(specs, asem.at[5], 1)
    total = specs[0]
    for i in range(1, DEVICES):
        total = total + specs[i]
    out_spec[...] = total
    wait_all(msgb, asem.at[0], 8)
    wait_all(msgc, asem.at[2], 16)
    wait_all(specs, asem.at[4], 1)
    for copy in sends:
        copy.wait_send()


def bin_tables(me, raw):
    pairs = [(d, 127 - d) for d in range(DEVICES)]
    mirrored = lax.ppermute(raw[:, 16:], AXES, pairs)
    single = jnp.where(me < 64, raw[:, 0], raw[:, 16])
    pairs = [(d, (64 if d == 0 else 128 - d) if d < 64 else 127 - d) for d in range(DEVICES)]
    extra = lax.ppermute(single, AXES, pairs)
    first = jnp.where(me < 64, raw[:, 16], jnp.where(me == 64, NBINS, raw[:, 0]))
    near = jnp.concatenate([first[:, None], raw[:, 1:16]], axis=1)
    far = jnp.concatenate([extra[:, None], mirrored[:, :0:-1]], axis=1)
    far = jnp.concatenate([far[:1], far[:0:-1]], axis=0)
    last = jnp.concatenate([raw[:, :1], jnp.full((N, 3), NBINS, jnp.int32)], axis=1)

    def arranged(cols):
        tiles = cols.shape[1] // 4
        return cols.reshape(32, 128, tiles, 4).transpose(2, 1, 0, 3).reshape(tiles, 128, 128)

    near = arranged(jnp.concatenate([near, last], axis=1))
    far = jnp.concatenate([arranged(far), jnp.full((1, 128, 128), NBINS, jnp.int32)], axis=0)
    return jnp.stack([near, far])


def on_device(tables, density, lens_weight, spectrum_bin):
    mats, ctw, rtw = tables
    bins = bin_tables(my_index(), spectrum_bin)
    vmem = pl.BlockSpec(memory_space=pltpu.VMEM)
    hbm = pl.BlockSpec(memory_space=pl.ANY)
    smem = pl.BlockSpec(memory_space=pltpu.SMEM)
    dma = pltpu.SemaphoreType.DMA
    share = (8, 4096)
    out = pl.pallas_call(
        kernel,
        name="shear",
        out_shape=(
            jax.ShapeDtypeStruct((32, N), F32),
            jax.ShapeDtypeStruct((32, N), F32),
            jax.ShapeDtypeStruct((1, 128), F32),
        ),
        in_specs=[hbm, smem, vmem, hbm, vmem, vmem],
        out_specs=(vmem, vmem, vmem),
        scratch_shapes=[
            pltpu.VMEM((256, N), F32),
            pltpu.VMEM((32, N), F32),
            pltpu.VMEM((6, 2, 256, 256), BF16),
            pltpu.VMEM((4, 2) + share, F32),
            pltpu.VMEM((4, 2) + share, F32),
            pltpu.VMEM((4, 2) + share, F32),
            pltpu.VMEM((4, 4) + share, F32),
            pltpu.VMEM((4, 4) + share, F32),
            pltpu.VMEM((2, 512, 128), F32),
            pltpu.VMEM((DEVICES * 8, 128), F32),
            pltpu.VMEM((DEVICES * 8, 128), F32),
            pltpu.VMEM((DEVICES * 16, 128), F32),
            pltpu.VMEM((DEVICES * 16, 128), F32),
            pltpu.VMEM((5, 128, 128), F32),
            pltpu.VMEM((128, 128), F32),
            pltpu.VMEM((1, 1, 128), F32),
            pltpu.VMEM((DEVICES, 1, 128), F32),
            dma((8,)),
            dma,
            dma((40,)),
            dma((40,)),
            dma((6,)),
        ],
        compiler_params=pltpu.CompilerParams(
            collective_id=0, has_side_effects=True, vmem_limit_bytes=60 * 1024 * 1024
        ),
    )(density, lens_weight, bins, mats, ctw, rtw)
    return out[0], out[1], out[2][0, :NBINS]


def solution(mesh):
    finer = Mesh(mesh.devices.reshape(4, 2, 2, 4, 2), AXES)
    tables = tuple(jnp.asarray(t) for t in make_tables())
    step = jax.shard_map(
        partial(on_device),
        mesh=finer,
        in_specs=((P(), P(), P()), P(PLANES, ROWS, None), P(PLANES), P(None, AXES)),
        out_specs=(P(AXES, None), P(AXES, None), P()),
        check_vma=False,
    )

    def whole(density, lens_weight, spectrum_bin):
        return step(tables, density, lens_weight, spectrum_bin)

    return whole
```

profile of v0, /device:TPU:1, one launch (start us, length us, event | category | flops | bytes accessed | tf_op | source)
XLA Modules:
  0.0 103.3 jit_solution(1139471155386835404)
XLA Ops:
  0.6 1.0 broadcast_select_fusion.2
  1.6 4.7 %collective-permute-start = (s32[4096]{0:T(1024)S(1)}, s32[4096]{0:T(1024)S(1)}, u32[]{:S(2)}, u32[]{:S(2)}) collective-permute-start(s32[4096]{0:T(1024)S(1)} %bitcast.34), channel_id=1, source_target_pairs={{0,64},{1,127},{2,126},{3,125},{4,124},{5,123},{6,122},{7,121},{8,... | collective-permute-start | bytes 49160 | tf_op jit(solution)/shard_map/ppermute | solution.py:515
  6.4 1.0 slice.30
  7.3 5.2 %collective-permute-start.1 = (s32[4096,16]{0,1:T(8,128)S(1)}, s32[4096,16]{0,1:T(8,128)S(1)}, u32[]{:S(2)}, u32[]{:S(2)}) collective-permute-start(s32[4096,16]{0,1:T(8,128)S(1)} %slice.30), channel_id=1, source_target_pairs={{0,127},{1,126},{2,125},{3,124},{4,123},{5,122},{6,121},{7,120},{8... | collective-permute-start | bytes 786440 | tf_op jit(solution)/shard_map/ppermute | solution.py:512
  12.6 1.0 slice.29
  13.6 0.1 pad.10.clone
  13.7 0.1 add_add_fusion
  14.4 0.1 copy.15
  14.5 0.2 copy.11
  14.8 0.2 copy.14
  14.9 5.7 %collective-permute-done.1 = s32[4096,16]{0,1:T(8,128)S(1)} collective-permute-done((s32[4096,16]{0,1:T(8,128)S(1)}, s32[4096,16]{0,1:T(8,128)S(1)}, u32[]{:S(2)}, u32[]{:S(2)}) %collective-permute-start.1) | collective-permute-done | bytes 262176 | tf_op jit(solution)/shard_map/ppermute | solution.py:512
  20.7 0.8 rev.6
  21.5 0.2 pad_add_fusion.1
  21.6 2.3 %reverse = s32[4096,16]{0,1:T(8,128)S(1)} reverse(s32[4096,16]{0,1:T(8,128)S(1)} %bitcast.29), dimensions={0} | reverse | bytes 524288
  23.9 0.2 slice.42
  24.1 0.1 add_bitcast_fusion
  24.2 0.1 copy.16
  24.3 0.2 copy.12
  24.5 0.1 copy.13
  24.6 0.9 pad_add_fusion.bins
  25.5 72.9 %shear.1 = (f32[32,4096]{1,0:T(8,128)}, f32[32,4096]{1,0:T(8,128)}, f32[1,128]{1,0:T(1,128)}) custom-call(f32[1,256,4096]{2,1,0:T(8,128)} %density.1, f32[1]{0:T(128)S(6)} %copy.19.weight, s32[2,5,128,128]{3,2,1,0:T(8,128)} %pad_add_fusion.bins, bf16[6,2,256,256]{3,2,1,0:T(8,128)(2,1)} %constant.33.clone.mats_in, f32[2,128,128]{2,1,0:T(8,128)} %constant.34.clone.ctw, ...), custom_call_target="tpu_custom_call" | custom-call | tf_op jit(solution)/shard_map/shear/pallas_call | solution.py:539
  98.5 1.1 %slice_bitcast_fusion = f32[64]{0:T(128)} fusion(f32[1,128]{1,0:T(1,128)} %get-tuple-element.8), kind=kLoop, calls=%fused_computation.9 | loop fusion | bytes 512 | tf_op jit(solution)/shard_map/squeeze | solution.py:577
  99.6 1.9 %copy.20 = f32[32,4096]{1,0:T(8,128)} copy(f32[32,4096]{1,0:T(8,128)} %get-tuple-element.15) | data formatting | bytes 1048576
  101.5 1.9 %copy.21 = f32[32,4096]{1,0:T(8,128)} copy(f32[32,4096]{1,0:T(8,128)} %get-tuple-element.16) | data formatting | bytes 1048576
  (6 shorter events, 0.1 us)
Async XLA Ops:
  1.6 19.8 %collective-permute-start = (s32[4096]{0:T(1024)S(1)}, s32[4096]{0:T(1024)S(1)}, u32[]{:S(2)}, u32[]{:S(2)}) collective-permute-start(s32[4096]{0:T(1024)S(1)} %bitcast.34), channel_id=1, source_target_pairs={{0,64},{1,127},{2,126},{3,125},{4,124},{5,123},{6,122},{7,121},{8,... | collective-permute-start | bytes 49160 | tf_op jit(solution)/shard_map/ppermute | solution.py:515
  7.3 13.3 %collective-permute-start.1 = (s32[4096,16]{0,1:T(8,128)S(1)}, s32[4096,16]{0,1:T(8,128)S(1)}, u32[]{:S(2)}, u32[]{:S(2)}) collective-permute-start(s32[4096,16]{0,1:T(8,128)S(1)} %slice.30), channel_id=1, source_target_pairs={{0,127},{1,126},{2,125},{3,124},{4,123},{5,122},{6,121},{7,120},{8... | collective-permute-start | bytes 786440 | tf_op jit(solution)/shard_map/ppermute | solution.py:512
where the time goes:
time: 104 us; the launch traced here: 103 us
  Pallas kernels  72.9 us (70%)
  local copies, waits for them, and re-layouts  11 us (11%)
  starting transfers between devices  9.95 us (10%)
  waiting for transfers between devices  5.72 us (6%)
  other arithmetic  2.3 us (2%)
  between operations  1.43 us (1%)
    pallas_call x1, Pallas kernels, on_device(): pl.pallas_call(kernel, name='shear', out_shape=(jax.ShapeDtypeStruct((32,...  72.9 us
    unnamed x7, local copies, waits for them, and re-layouts  6.34 us
    ppermute x1, waiting for transfers between devices, bin_tables(): mirrored = lax.ppermute(raw[:, 16:], AXES, pairs)  5.72 us
    ppermute x1, starting transfers between devices, bin_tables(): mirrored = lax.ppermute(raw[:, 16:], AXES, pairs)  5.22 us
    ppermute x1, starting transfers between devices, bin_tables(): extra = lax.ppermute(single, AXES, pairs)  4.73 us
  transfers between devices with their start and end apart: 2, of which 1 were waited for; matrix products, arithmetic and copies ran while one was open for 3% of the time, Pallas kernels for 0%

commit v1 on v0

--- a/solution.py
+++ b/solution.py
@@ -69,10 +69,19 @@
     column_twiddle = np.stack([np.cos(phase), np.sin(phase)]).astype(np.float32)
     phase = turn * (np.arange(16)[:, None] * i128[None, :]) / 4096
     row_twiddle = np.stack([np.cos(phase), np.sin(phase)]).astype(np.float32)
-    return mats, column_twiddle, row_twiddle
-
-
-FORWARD, INVERSE, FIRST, BACK, LANES, LANES_BACK = range(6)
+    extra = np.zeros((1, 2, 256, 256), ml_dtypes.bfloat16)
+    for c in range(2):
+        for j, (up, left) in enumerate(((0, 0), (0, 128), (128, 0))):
+            part = column_twiddle[c].astype(ml_dtypes.bfloat16)
+            column_twiddle[c] -= part.astype(np.float32)
+            extra[0, c, up : up + 128, left : left + 128] = part
+            part = row_twiddle[c].astype(ml_dtypes.bfloat16)
+            row_twiddle[c] -= part.astype(np.float32)
+            extra[0, c, 128 + 16 * j : 144 + 16 * j, 128:] = part
+    return np.concatenate([mats, extra])
+
+
+FORWARD, INVERSE, FIRST, BACK, LANES, LANES_BACK, TWIDDLES = range(7)
 
 
 def rfft(values):
@@ -135,6 +144,20 @@
     high, low = split(data)
     dot = partial(jnp.dot, preferred_element_type=F32)
     return dot(high, mats[which, 0]) + dot(low, mats[which, 0]) + dot(high, mats[which, 1])
+
+
+def read_twiddles(mats, ctw, rtw):
+    for c in range(2):
+        parts = [
+            mats[TWIDDLES, c, pl.ds(up, 128), pl.ds(left, 128)].astype(F32)
+            for up, left in ((0, 0), (0, 128), (128, 0))
+        ]
+        ctw[c] = parts[0] + parts[1] + parts[2]
+        parts = [
+            mats[TWIDDLES, c, pl.ds(128 + 16 * j, 16), pl.ds(128, 128)].astype(F32)
+            for j in range(3)
+        ]
+        rtw[c] = parts[0] + parts[1] + parts[2]
 
 
 def my_index():
@@ -277,9 +300,16 @@
                 outs[ac][pl.ds(q * 8, 8), pl.ds(x1 * 128, 128)] = out[x1]
 
 
+STRIDE = 37
+
+
+def peer(me, i):
+    return lax.rem(me + i * STRIDE, DEVICES)
+
+
 def send_all(me, msg, recv, send, arrive, rows):
     def step(i, _):
-        to = lax.rem(me + i, DEVICES)
+        to = peer(me, i)
         pltpu.make_async_remote_copy(
             src_ref=msg.at[pl.ds(pl.multiple_of(to * rows, rows), rows)],
             dst_ref=recv.at[pl.ds(pl.multiple_of(me * rows, rows), rows)],
@@ -300,7 +330,42 @@
     pltpu.make_async_copy(part, part, sem).wait()
 
 
-def bin_power(bins, power, acc, spec):
+def arrange_bins(me, raw, near, far):
+    row = lax.broadcasted_iota(jnp.int32, (128, 128), 0)
+    lane = lax.broadcasted_iota(jnp.int32, (128, 128), 1)
+    rcol, rky2 = row % 32, row // 32
+    lcol, lky2 = lane % 4, lane // 4
+    low = me < 64
+    wanted = []
+    for t in range(4):
+        slot = 4 * t + lcol
+        own, other = slot, 32 - slot
+        if t == 0:
+            own = jnp.where(slot == 0, jnp.where(low, 16, 0), own)
+            other = jnp.where(slot == 0, jnp.where(low, 0, 16), other)
+        wanted.append((rcol == own, lky2 - rky2))
+        wanted.append((rcol == other, 31 - lky2 - rky2))
+    wanted.append((jnp.logical_and(lcol == 0, rcol == 0), lky2 - rky2))
+    sums = [jnp.zeros((128, 128), F32) for _ in wanted]
+    for g in range(8):
+        pieces = [raw[:, pl.ds((4 * g + i) * 128, 128)].astype(F32) for i in range(4)]
+        data = jnp.concatenate(pieces, axis=0).T.astype(BF16)
+        for i, (match, shift) in enumerate(wanted):
+            pick = jnp.where(jnp.logical_and(match, shift == 4 * g), 1.0, 0.0).astype(BF16)
+            sums[i] = sums[i] + jnp.dot(data, pick, preferred_element_type=F32)
+    flip = jnp.where(jnp.logical_and(row + lane == 128, row > 0), 1.0, 0.0).astype(BF16)
+    for t in range(4):
+        own, other = sums[2 * t], sums[2 * t + 1]
+        if t == 0:
+            own = jnp.where(jnp.logical_and(lcol == 0, me == 64), float(NBINS), own)
+        near[t] = own
+        turned = jnp.dot(flip, other.astype(BF16), preferred_element_type=F32)
+        first = jnp.concatenate([other[:1, 124:], other[:1, :124]], axis=1)
+        far[t] = jnp.where(row == 0, first, turned)
+    near[4] = sums[8]
+
+
+def bin_power(near, far, power, acc, spec):
     def group(g, _):
         sums = [jnp.zeros((8, 128), F32) for _ in range(8)]
         for i in range(9):
@@ -308,10 +373,10 @@
             which = 0 if i < 5 else 1
             for r in range(16):
                 at = pl.ds(r * 8, 8)
-                b = bins[which, t, at, :] - g * 8
+                b = (far if which else near)[t, at, :] - (g * 8).astype(F32)
                 p = power[t, at, :]
                 for k in range(8):
-                    sums[k] = sums[k] + jnp.where(b == k, p, 0.0)
+                    sums[k] = sums[k] + jnp.where(b == float(k), p, 0.0)
         rows = [jnp.sum(v, axis=0, keepdims=True) for v in sums]
         acc[pl.ds(pl.multiple_of(g * 8, 8), 8), :] = jnp.concatenate(rows, axis=0)
         return 0
@@ -322,7 +387,7 @@
     spec[0] = row * (NBINS / float(N) ** 4)
 
 
-def reduce_planes(weight, mine, res, yf, zf, yrelay, ydirect, yfinal, zrecv, zsum, ssem, rsem):
+def reduce_planes(idle, mine, res, yf, zf, yrelay, ydirect, yfinal, zrecv, zsum, ssem, rsem):
     y, zh = lax.axis_index("y"), lax.axis_index("zh")
     base = my_index() - y * 2 - zh
     up, down, across = lax.rem(y + 1, 4), lax.rem(y + 3, 4), lax.rem(y + 2, 4)
@@ -423,6 +488,7 @@
             )
 
     y_relay_first(yf[0])
+    idle()
     y_relay_first(yf[1])
     y_finish_first(yf[0])
     z_first(zf[0])
@@ -438,10 +504,10 @@
 
 
 def kernel(
-    density, weight, bins, mats_in, ctw, rtw, out_real, out_imag, out_spec,
-    mine, res, mats, yrelay, ydirect, yfinal, zrecv, zsum,
-    ubuf, msgb, recvb, msgc, recvc, power, acc, spec, specs,
-    lsem, msem, ssem, rsem, asem,
+    density, weight, bins_in, mats_in, out_real, out_imag, out_spec,
+    recvc, specs, ctw, rtw, mine, res, mats, yrelay, ydirect, yfinal, zrecv, zsum,
+    ubuf, msgb, recvb, msgc, power, acc, spec, raw, near, far, farin, extra,
+    lsem, msem, bsem, fsem, ssem, rsem, asem,
 ):
     me = my_index()
     barrier = pltpu.get_barrier_semaphore()
@@ -454,6 +520,8 @@
         loads.append(copy)
     mload = pltpu.make_async_copy(mats_in, mats, msem)
     mload.start()
+    bload = pltpu.make_async_copy(bins_in, raw, bsem)
+    bload.start()
 
     def greet(i, _):
         pl.semaphore_signal(
@@ -468,19 +536,55 @@
         rows = pl.ds(i * 32, 32)
         mine[rows, :] = mine[rows, :] * w
     pl.semaphore_wait(barrier, DEVICES - 1)
+
+    def idle():
+        mload.wait()
+        read_twiddles(mats, ctw, rtw)
+        bload.wait()
+        arrange_bins(me, raw, near, far)
+
     sends = reduce_planes(
-        weight, mine, res, (0, 1), (2, 3), yrelay, ydirect, yfinal, zrecv, zsum, ssem, rsem
+        idle, mine, res, (0, 1), (2, 3), yrelay, ydirect, yfinal, zrecv, zsum, ssem, rsem
     )
-    mload.wait()
     row_forward(res, mats, rtw, ubuf, msgb)
     send_all(me, msgb, recvb, asem.at[0], asem.at[1], 8)
+    mirror = pltpu.make_async_remote_copy(
+        src_ref=far,
+        dst_ref=farin,
+        send_sem=fsem.at[0],
+        recv_sem=fsem.at[1],
+        device_id=DEVICES - 1 - me,
+        device_id_type=LOGICAL,
+    )
+    mirror.start()
+    zeroth = pltpu.make_async_remote_copy(
+        src_ref=far.at[0],
+        dst_ref=extra,
+        send_sem=fsem.at[2],
+        recv_sem=fsem.at[3],
+        device_id=jnp.where(me == 0, 64, DEVICES - me),
+        device_id_type=LOGICAL,
+    )
+
+    @pl.when(me < 64)
+    def _():
+        zeroth.start()
+
     wait_all(recvb, asem.at[1], 8)
     column_part(me, recvb, mats, ctw, power, msgc)
     send_all(me, msgc, recvc, asem.at[2], asem.at[3], 16)
-    bin_power(bins, power, acc, spec)
+    mirror.wait_recv()
+
+    @pl.when(me >= 64)
+    def _():
+        zeroth.wait_recv()
+        lane = lax.broadcasted_iota(jnp.int32, (128, 128), 1)
+        farin[0] = jnp.where(lane % 4 == 0, extra[...], farin[0])
+
+    bin_power(near, farin, power, acc, spec)
 
     def share_spec(i, _):
-        to = lax.rem(me + i, DEVICES)
+        to = peer(me, i)
         pltpu.make_async_remote_copy(
             src_ref=spec.at[0],
             dst_ref=specs.at[me],
@@ -499,57 +603,54 @@
     total = specs[0]
     for i in range(1, DEVICES):
         total = total + specs[i]
-    out_spec[...] = total
+    out_spec[...] = total[:, :NBINS]
     wait_all(msgb, asem.at[0], 8)
     wait_all(msgc, asem.at[2], 16)
     wait_all(specs, asem.at[4], 1)
     for copy in sends:
         copy.wait_send()
-
-
-def bin_tables(me, raw):
-    pairs = [(d, 127 - d) for d in range(DEVICES)]
-    mirrored = lax.ppermute(raw[:, 16:], AXES, pairs)
-    single = jnp.where(me < 64, raw[:, 0], raw[:, 16])
-    pairs = [(d, (64 if d == 0 else 128 - d) if d < 64 else 127 - d) for d in range(DEVICES)]
-    extra = lax.ppermute(single, AXES, pairs)
-    first = jnp.where(me < 64, raw[:, 16], jnp.where(me == 64, NBINS, raw[:, 0]))
-    near = jnp.concatenate([first[:, None], raw[:, 1:16]], axis=1)
-    far = jnp.concatenate([extra[:, None], mirrored[:, :0:-1]], axis=1)
-    far = jnp.concatenate([far[:1], far[:0:-1]], axis=0)
-    last = jnp.concatenate([raw[:, :1], jnp.full((N, 3), NBINS, jnp.int32)], axis=1)
-
-    def arranged(cols):
-        tiles = cols.shape[1] // 4
-        return cols.reshape(32, 128, tiles, 4).transpose(2, 1, 0, 3).reshape(tiles, 128, 128)
-
-    near = arranged(jnp.concatenate([near, last], axis=1))
-    far = jnp.concatenate([arranged(far), jnp.full((1, 128, 128), NBINS, jnp.int32)], axis=0)
-    return jnp.stack([near, far])
-
-
-def on_device(tables, density, lens_weight, spectrum_bin):
-    mats, ctw, rtw = tables
-    bins = bin_tables(my_index(), spectrum_bin)
+    mirror.wait_send()
+
+    @pl.when(me < 64)
+    def _():
+        zeroth.wait_send()
+
+
+def finish(*refs):
+    sems = refs[6]
+    copies = [pltpu.make_async_copy(refs[i], refs[3 + i], sems.at[i]) for i in range(3)]
+    for copy in copies:
+        copy.start()
+    for copy in copies:
+        copy.wait()
+
+
+def on_device(mats, density, lens_weight, spectrum_bin):
     vmem = pl.BlockSpec(memory_space=pltpu.VMEM)
-    hbm = pl.BlockSpec(memory_space=pl.ANY)
+    hbm = pl.BlockSpec(memory_space=pltpu.HBM)
     smem = pl.BlockSpec(memory_space=pltpu.SMEM)
     dma = pltpu.SemaphoreType.DMA
     share = (8, 4096)
-    out = pl.pallas_call(
+    params = partial(pltpu.CompilerParams, vmem_limit_bytes=55050240)
+    shapes = (
+        jax.ShapeDtypeStruct((32, N), F32),
+        jax.ShapeDtypeStruct((32, N), F32),
+        jax.ShapeDtypeStruct((1, NBINS), F32),
+    )
+    results = pl.pallas_call(
         kernel,
         name="shear",
-        out_shape=(
-            jax.ShapeDtypeStruct((32, N), F32),
-            jax.ShapeDtypeStruct((32, N), F32),
-            jax.ShapeDtypeStruct((1, 128), F32),
-        ),
-        in_specs=[hbm, smem, vmem, hbm, vmem, vmem],
+        out_shape=shapes,
+        in_specs=[hbm, smem, hbm, hbm],
         out_specs=(vmem, vmem, vmem),
         scratch_shapes=[
+            pltpu.VMEM((DEVICES * 16, 128), F32),
+            pltpu.VMEM((DEVICES, 1, 128), F32),
+            pltpu.VMEM((2, 128, 128), F32),
+            pltpu.VMEM((2, 16, 128), F32),
             pltpu.VMEM((256, N), F32),
             pltpu.VMEM((32, N), F32),
-            pltpu.VMEM((6, 2, 256, 256), BF16),
+            pltpu.VMEM((7, 2, 256, 256), BF16),
             pltpu.VMEM((4, 2) + share, F32),
             pltpu.VMEM((4, 2) + share, F32),
             pltpu.VMEM((4, 2) + share, F32),
@@ -559,31 +660,43 @@
             pltpu.VMEM((DEVICES * 8, 128), F32),
             pltpu.VMEM((DEVICES * 8, 128), F32),
             pltpu.VMEM((DEVICES * 16, 128), F32),
-            pltpu.VMEM((DEVICES * 16, 128), F32),
             pltpu.VMEM((5, 128, 128), F32),
             pltpu.VMEM((128, 128), F32),
             pltpu.VMEM((1, 1, 128), F32),
-            pltpu.VMEM((DEVICES, 1, 128), F32),
+            pltpu.VMEM((32, N), jnp.int32),
+            pltpu.VMEM((5, 128, 128), F32),
+            pltpu.VMEM((4, 128, 128), F32),
+            pltpu.VMEM((4, 128, 128), F32),
+            pltpu.VMEM((128, 128), F32),
             dma((8,)),
             dma,
+            dma,
+            dma((4,)),
             dma((40,)),
             dma((40,)),
             dma((6,)),
         ],
-        compiler_params=pltpu.CompilerParams(
-            collective_id=0, has_side_effects=True, vmem_limit_bytes=60 * 1024 * 1024
-        ),
-    )(density, lens_weight, bins, mats, ctw, rtw)
-    return out[0], out[1], out[2][0, :NBINS]
+        compiler_params=params(collective_id=0, has_side_effects=True),
+    )(density, lens_weight, spectrum_bin.T, mats)
+    real, imag, spectrum = pl.pallas_call(
+        finish,
+        name="finish",
+        out_shape=shapes,
+        in_specs=[vmem, vmem, vmem],
+        out_specs=(hbm, hbm, hbm),
+        scratch_shapes=[dma((3,))],
+        compiler_params=params(),
+    )(*results)
+    return real, imag, spectrum.reshape(NBINS)
 
 
 def solution(mesh):
     finer = Mesh(mesh.devices.reshape(4, 2, 2, 4, 2), AXES)
-    tables = tuple(jnp.asarray(t) for t in make_tables())
+    tables = jnp.asarray(make_tables())
     step = jax.shard_map(
-        partial(on_device),
+        on_device,
         mesh=finer,
-        in_specs=((P(), P(), P()), P(PLANES, ROWS, None), P(PLANES), P(None, AXES)),
+        in_specs=(P(), P(PLANES, ROWS, None), P(PLANES), P(None, AXES)),
         out_specs=(P(AXES, None), P(AXES, None), P()),
         check_vma=False,
     )

time: 104 us -> 76.7 us (0.74)
  local copies, waits for them, and re-layouts: 11 us -> 0 us
  starting transfers between devices: 9.95 us -> 0 us
  waiting for transfers between devices: 5.72 us -> 0 us
  Pallas kernels: 72.9 us -> 75.3 us
  other arithmetic: 2.3 us -> 0 us
    ppermute x2 -> x0, starting transfers between devices: 9.95 us -> none  [the longest x1 5.22 us: bin_tables(): mirrored = lax.ppermute(raw[:, 16:], AXES, pairs)]
    unnamed x7 -> x0, local copies, waits for them, and re-layouts: 6.34 us -> none
    ppermute x2 -> x0, waiting for transfers between devices: 5.72 us -> none  [the longest x1 5.72 us: bin_tables(): mirrored = lax.ppermute(raw[:, 16:], AXES, pairs)]
    pallas_call x1 -> x2, Pallas kernels: 72.9 us -> 75.3 us  [the longest x1 74.3 us: on_device(): pl.pallas_call(kernel, name='shear', out_shape=shapes, in_specs=[hbm, sme...]
    slice x3 -> x0, local copies, waits for them, and re-layouts: 2.01 us -> none  [the longest x1 1.02 us: bin_tables(): near = jnp.concatenate([first[:, None], raw[:, 1:16]], axis=1)]
    squeeze x1 -> x0, local copies, waits for them, and re-layouts: 1.14 us -> none  [on_device(): return (out[0], out[1], out[2][0, :NBINS])]
  transfers between devices with their start and end apart: 2 -> 0, of which waited for: 1 -> 0; matrix products, arithmetic and copies ran while one was open for 3% -> 0% of each run, Pallas kernels for 0% -> 0%
where the time goes in v1:
time: 76.7 us; the launch traced here: 76.6 us
  Pallas kernels  75.3 us (98%)
  between operations  1.28 us (2%)
    pallas_call x1, Pallas kernels, on_device(): pl.pallas_call(kernel, name='shear', out_shape=shapes, in_specs=[hbm, sme...  74.3 us

profile of v1, /device:TPU:1, one launch (start us, length us, event | category | flops | bytes accessed | tf_op | source)
XLA Modules:
  0.0 76.6 jit_solution(11103327443144752563)
XLA Ops:
  1.3 74.3 %shear.1 = (f32[32,4096]{1,0:T(8,128)S(1)}, f32[32,4096]{1,0:T(8,128)S(1)}, f32[1,64]{1,0:T(1,128)S(1)}) custom-call(f32[1,256,4096]{2,1,0:T(8,128)} %density.1, f32[1]{0:T(128)S(6)} %copy.7.weight, s32[32,4096]{1,0:T(8,128)} %bitcast.2, bf16[7,2,256,256]{3,2,1,0:T(8,128)(2,1)} %constant.2.clone.mats_in), custom_call_target="tpu_custom_call" | custom-call | tf_op jit(solution)/shard_map/shear/pallas_call | solution.py:640
  75.6 1.0 %finish.1 = (f32[32,4096]{1,0:T(8,128)}, f32[32,4096]{1,0:T(8,128)}, f32[1,64]{1,0:T(1,128)}) custom-call(f32[32,4096]{1,0:T(8,128)S(1)} %get-tuple-element.9.refs_0_, f32[32,4096]{1,0:T(8,128)S(1)} %get-tuple-element.10.refs_1_, f32[1,64]{1,0:T(1,128)S(1)} %get-tuple-element.11.refs_2_), custom_call_target="tpu_custom_call" | custom-call | tf_op jit(solution)/shard_map/finish/pallas_call | solution.py:681

commit v2 on v1

--- a/solution.py
+++ b/solution.py
@@ -165,10 +165,10 @@
     return ((x * 2 + zl) * 2 + core) * 8 + y * 2 + zh
 
 
-def row_forward(res, mats, rtw, ubuf, msg):
+def row_forward(b, w, mine, mats, rtw, ubuf, spread):
     for q in range(4):
-        rows = pl.ds(q * 8, 8)
-        out = rfft([res[rows, pl.ds(x1 * 128, 128)] for x1 in range(32)])
+        rows = pl.ds(b * 32 + q * 8, 8)
+        out = rfft([mine[rows, pl.ds(x1 * 128, 128)] * w for x1 in range(32)])
         for k1 in range(16):
             at = pl.ds(k1 * 32 + q * 8, 8)
             if k1 == 0:
@@ -179,18 +179,20 @@
                 ubuf[0, at, :] = ur * tr + ui * ti
                 ubuf[1, at, :] = ui * tr - ur * ti
     data = jnp.concatenate([ubuf[0].T, ubuf[1].T], axis=0)
-    spread = table_times(mats, FORWARD, data)
+    out = table_times(mats, FORWARD, data)
     special = table_times(mats, FIRST, data[:, :128])
     lane = lax.broadcasted_iota(jnp.int32, (256, 128), 1)
     for t in range(4):
-        piece = spread[:, t * 128 : (t + 1) * 128]
+        piece = out[:, t * 128 : (t + 1) * 128]
         if t == 0:
             piece = jnp.where(lane < 32, special, piece)
         for c in range(2):
-            msg[pl.ds(c * 4 + t, 128, stride=8), :] = piece[c * 128 : (c + 1) * 128]
-
-
-def column_part(me, recv, mats, ctw, power, msg):
+            for r in range(16):
+                at = c * 128 + r * 8
+                spread[pl.ds(b * 1024 + r * 8 + c * 4 + t, 8, stride=128), :] = piece[at : at + 8]
+
+
+def column_part(me, recv, mats, ctw, power, msg, send):
     lane = lax.broadcasted_iota(jnp.int32, (128, 128), 1)
     sub = lax.broadcasted_iota(jnp.int32, (128, 128), 0)
     special = jnp.logical_and(lane < 32, me == 64)
@@ -248,71 +250,72 @@
             a = (kr * fr - ki * fi, kr * fi + ki * fr)
             c = (kn * fr, kn * fi)
         hats.append((a, c))
-    rows = [jnp.concatenate(hats[t][ac], axis=1) for ac in range(2) for t in range(5)]
-    g = times_table(mats, LANES_BACK, jnp.concatenate(rows, axis=0))
-    re, im = [], []
-    for i in range(10):
-        gr, gi = g[i * 128 : (i + 1) * 128, :128], g[i * 128 : (i + 1) * 128, 128:]
-        re.append(gr * tc - gi * ts)
-        im.append(gi * tc + gr * ts)
-    data = jnp.concatenate([jnp.concatenate(re, axis=1), jnp.concatenate(im, axis=1)], axis=0)
-    s = table_times(mats, INVERSE, data)
     for ac in range(2):
+        rows = [jnp.concatenate(hats[t][ac], axis=1) for t in range(5)]
+        g = times_table(mats, LANES_BACK, jnp.concatenate(rows, axis=0))
+        re, im = [], []
+        for t in range(5):
+            gr, gi = g[t * 128 : (t + 1) * 128, :128], g[t * 128 : (t + 1) * 128, 128:]
+            re.append(gr * tc - gi * ts)
+            im.append(gi * tc + gr * ts)
+        data = jnp.concatenate([jnp.concatenate(re, axis=1), jnp.concatenate(im, axis=1)], axis=0)
+        s = table_times(mats, INVERSE, data)
         for t in range(4):
-            at = (ac * 5 + t) * 128
-            sr, si = s[:128, at : at + 128], s[128:, at : at + 128]
+            sr, si = s[:128, t * 128 : (t + 1) * 128], s[128:, t * 128 : (t + 1) * 128]
             if t == 0:
-                extra = (ac * 5 + 4) * 128
-                si = jnp.where(special, s[:128, extra : extra + 128], si)
-            msg[pl.ds(ac * 8 + t, 128, stride=16), :] = sr
-            msg[pl.ds(ac * 8 + 4 + t, 128, stride=16), :] = si
-
-
-def row_inverse(recv, mats, rtw, vbuf, outs):
+                si = jnp.where(special, s[:128, 512:], si)
+            msg[pl.ds(ac * 1024 + t, 128, stride=8), :] = sr
+            msg[pl.ds(ac * 1024 + 4 + t, 128, stride=8), :] = si
+        send(ac)
+
+
+def row_inverse(ac, recv, mats, rtw, vbuf, out_ref):
     lane = lax.broadcasted_iota(jnp.int32, (256, 128), 1)
-    for ac in range(2):
-        parts = [
-            jnp.concatenate(
-                [recv[pl.ds(ac * 8 + c * 4 + t, 128, stride=16), :] for t in range(4)], axis=1
-            )
-            for c in range(2)
-        ]
-        data = jnp.concatenate(parts, axis=0)
-        v = table_times(mats, INVERSE, data)
-        special = table_times(mats, BACK, data[:, :128])
-        first = jnp.where(lane < 32, special, v[:, :128])
-        for c in range(2):
-            rows = slice(c * 128, (c + 1) * 128)
-            full = jnp.concatenate([first[rows], v[rows, 128:]], axis=1)
-            vbuf[c] = full.T
-        for q in range(4):
-            g = [None] * 17
-            for k1 in range(16):
-                at = pl.ds(k1 * 32 + q * 8, 8)
-                vr, vi = vbuf[0, at, :], vbuf[1, at, :]
-                if k1 == 0:
-                    g[0], g[16] = (vr, None), (vi, None)
-                else:
-                    tr, ti = rtw[0, pl.ds(k1, 1), :], rtw[1, pl.ds(k1, 1), :]
-                    g[k1] = (vr * tr - vi * ti, vi * tr + vr * ti)
-            out = irfft(g)
-            for x1 in range(32):
-                outs[ac][pl.ds(q * 8, 8), pl.ds(x1 * 128, 128)] = out[x1]
-
-
-STRIDE = 37
+    parts = [
+        jnp.concatenate(
+            [recv[pl.ds(ac * 1024 + c * 4 + t, 128, stride=8), :] for t in range(4)], axis=1
+        )
+        for c in range(2)
+    ]
+    data = jnp.concatenate(parts, axis=0)
+    v = table_times(mats, INVERSE, data)
+    special = table_times(mats, BACK, data[:, :128])
+    first = jnp.where(lane < 32, special, v[:, :128])
+    for c in range(2):
+        rows = slice(c * 128, (c + 1) * 128)
+        full = jnp.concatenate([first[rows], v[rows, 128:]], axis=1)
+        vbuf[c] = full.T
+    for q in range(4):
+        g = [None] * 17
+        for k1 in range(16):
+            at = pl.ds(k1 * 32 + q * 8, 8)
+            vr, vi = vbuf[0, at, :], vbuf[1, at, :]
+            if k1 == 0:
+                g[0], g[16] = (vr, None), (vi, None)
+            else:
+                tr, ti = rtw[0, pl.ds(k1, 1), :], rtw[1, pl.ds(k1, 1), :]
+                g[k1] = (vr * tr - vi * ti, vi * tr + vr * ti)
+        out = irfft(g)
+        for x1 in range(32):
+            out_ref[pl.ds(q * 8, 8), pl.ds(x1 * 128, 128)] = out[x1]
+
+
+STRIDE = 107
 
 
 def peer(me, i):
     return lax.rem(me + i * STRIDE, DEVICES)
 
 
-def send_all(me, msg, recv, send, arrive, rows):
+def send_all(me, half, msg, recv, send, arrive):
+    def block(d):
+        return pl.ds(pl.multiple_of((half * DEVICES + d) * 8, 8), 8)
+
     def step(i, _):
         to = peer(me, i)
         pltpu.make_async_remote_copy(
-            src_ref=msg.at[pl.ds(pl.multiple_of(to * rows, rows), rows)],
-            dst_ref=recv.at[pl.ds(pl.multiple_of(me * rows, rows), rows)],
+            src_ref=msg.at[block(to)],
+            dst_ref=recv.at[block(me)],
             send_sem=send,
             recv_sem=arrive,
             device_id=to,
@@ -321,12 +324,11 @@
         return 0
 
     lax.fori_loop(1, DEVICES, step, 0)
-    own = pl.ds(pl.multiple_of(me * rows, rows), rows)
-    recv[own, :] = msg[own, :]
-
-
-def wait_all(buf, sem, rows):
-    part = buf.at[pl.ds(0, (DEVICES - 1) * rows)]
+    recv[block(me), :] = msg[block(me), :]
+
+
+def wait_all(buf, sem, rows, count=DEVICES - 1):
+    part = buf.at[pl.ds(0, count * rows)]
     pltpu.make_async_copy(part, part, sem).wait()
 
 
@@ -387,126 +389,108 @@
     spec[0] = row * (NBINS / float(N) ** 4)
 
 
-def reduce_planes(idle, mine, res, yf, zf, yrelay, ydirect, yfinal, zrecv, zsum, ssem, rsem):
-    y, zh = lax.axis_index("y"), lax.axis_index("zh")
-    base = my_index() - y * 2 - zh
-    up, down, across = lax.rem(y + 1, 4), lax.rem(y + 3, 4), lax.rem(y + 2, 4)
-    dev_up, dev_down = base + up * 2 + zh, base + down * 2 + zh
-    dev_z = base + y * 2 + (1 - zh)
-    count = [0]
-    sends = []
-
-    def send(src, dst, to):
-        i = count[0]
-        count[0] += 1
+class Reduction:
+    def __init__(self, spread, total, yrelay, ydirect, yfinal, zrecv, zsum, ssem, rsem):
+        self.spread, self.total, self.zrecv, self.zsum = spread, total, zrecv, zsum
+        self.yrelay, self.ydirect, self.yfinal = yrelay, ydirect, yfinal
+        self.ssem, self.rsem, self.sends = ssem, rsem, []
+        y, zh = lax.axis_index("y"), lax.axis_index("zh")
+        base = my_index() - y * 2 - zh
+        up, down, across = lax.rem(y + 1, 4), lax.rem(y + 3, 4), lax.rem(y + 2, 4)
+        self.y, self.zh, self.turn = y, zh, (across, up, down, y)
+        self.dev_up, self.dev_down = base + up * 2 + zh, base + down * 2 + zh
+        self.dev_z = base + y * 2 + (1 - zh)
+        self.moves = {}
+
+    def send(self, key, src, dst, to):
+        i = len(self.sends)
         copy = pltpu.make_async_remote_copy(
             src_ref=src,
             dst_ref=dst,
-            send_sem=ssem.at[i],
-            recv_sem=rsem.at[i],
+            send_sem=self.ssem.at[i],
+            recv_sem=self.rsem.at[i],
             device_id=to,
             device_id_type=LOGICAL,
         )
         copy.start()
-        sends.append(copy)
-        return copy
-
-    def share(t, h, q):
-        return mine.at[pl.ds(pl.multiple_of((t * 2 + h) * 32 + q * 8, 8), 8)]
-
-    znew = {}
-    for q in zf:
-        for i, t in enumerate((across, up, down, y)):
-            znew[q, i] = send(share(t, 1 - zh, q), zrecv.at[q, i], dev_z)
-    relay, direct, final = {}, {}, {}
-    for q in yf:
-        relay[q, 0] = send(share(across, 0, q), yrelay.at[q, 0], dev_up)
-        relay[q, 1] = send(share(across, 1, q), yrelay.at[q, 1], dev_down)
-        direct[q, 0] = send(share(up, 1, q), ydirect.at[q, 1], dev_up)
-        direct[q, 1] = send(share(down, 0, q), ydirect.at[q, 0], dev_down)
-    half = (slice(0, 2048), slice(2048, 4096))
-
-    def y_relay_first(q):
-        relay[q, 0].wait_recv()
-        yrelay[q, 0] = yrelay[q, 0] + share(up, 0, q)[...]
-        final[q, 0] = send(yrelay.at[q, 0], yfinal.at[q, 0], dev_up)
-        relay[q, 1].wait_recv()
-        yrelay[q, 1] = yrelay[q, 1] + share(down, 1, q)[...]
-        final[q, 1] = send(yrelay.at[q, 1], yfinal.at[q, 1], dev_down)
-
-    def y_finish_first(q):
+        self.sends.append(copy)
+        self.moves[key] = copy
+
+    def arrived(self, *keys):
+        for key in keys:
+            self.moves[key].wait_recv()
+
+    def share(self, t, h, b):
+        return self.spread.at[pl.ds(pl.multiple_of(b * 1024 + (t * 2 + h) * 128, 128), 128)]
+
+
+    def y_start(self, b):
+        across, up, down, _ = self.turn
+        self.send(("relay", b, 0), self.share(across, 0, b), self.yrelay.at[b, 0], self.dev_up)
+        self.send(("relay", b, 1), self.share(across, 1, b), self.yrelay.at[b, 1], self.dev_down)
+        self.send(("direct", b, 0), self.share(up, 1, b), self.ydirect.at[b, 1], self.dev_up)
+        self.send(("direct", b, 1), self.share(down, 0, b), self.ydirect.at[b, 0], self.dev_down)
+
+    def y_relay(self, b):
+        for h, t, to in ((0, self.turn[1], self.dev_up), (1, self.turn[2], self.dev_down)):
+            self.arrived(("relay", b, h))
+            self.yrelay[b, h] = self.yrelay[b, h] + self.share(t, h, b)[...]
+            self.send(("final", b, h), self.yrelay.at[b, h], self.yfinal.at[b, h], to)
+
+    def y_finish(self, b):
+        self.arrived(("direct", b, 0), ("direct", b, 1), ("final", b, 0), ("final", b, 1))
         for h in range(2):
-            direct[q, h].wait_recv()
-            final[q, h].wait_recv()
+            own = self.share(self.y, h, b)[...]
+            self.yfinal[b, h] = self.yfinal[b, h] + self.ydirect[b, h] + own
+        self.send(("z", b, 0), self.yfinal.at[b, 1 - self.zh], self.zrecv.at[b, 0], self.dev_z)
+
+    def z_last(self, b):
+        self.arrived(("z", b, 0))
+        self.total[b] = self.zrecv[b, 0] + self.yfinal[b, self.zh]
+
+
+    def z_start(self, b):
+        for i, t in enumerate(self.turn):
+            self.send(("z", b, i), self.share(t, 1 - self.zh, b), self.zrecv.at[b, i], self.dev_z)
+
+    def z_then_y(self, b):
+        low, high = pl.ds(0, 64), pl.ds(64, 64)
+        zsum = self.zsum
+        for i, t in enumerate(self.turn):
+            self.arrived(("z", b, i))
+            zsum[b, i] = self.zrecv[b, i] + self.share(t, self.zh, b)[...]
+            if i == 0:
+                up, down = self.yrelay.at[b, 0, low], self.yrelay.at[b, 1, low]
+                self.send(("relay", b, 0), zsum.at[b, 0, low], up, self.dev_up)
+                self.send(("relay", b, 1), zsum.at[b, 0, high], down, self.dev_down)
+            if i == 1:
+                up = self.ydirect.at[b, 1, low]
+                self.send(("direct", b, 0), zsum.at[b, 1, high], up, self.dev_up)
+            if i == 2:
+                down = self.ydirect.at[b, 0, low]
+                self.send(("direct", b, 1), zsum.at[b, 2, low], down, self.dev_down)
+
+    def y_relay_half(self, b):
+        low = pl.ds(0, 64)
+        for h, i, to in ((0, 1, self.dev_up), (1, 2, self.dev_down)):
+            self.arrived(("relay", b, h))
+            own = self.zsum[b, i, pl.ds(h * 64, 64)]
+            self.yrelay[b, h, low] = self.yrelay[b, h, low] + own
+            self.send(("final", b, h), self.yrelay.at[b, h, low], self.yfinal.at[b, h, low], to)
+
+    def y_last(self, b):
+        self.arrived(("direct", b, 0), ("direct", b, 1), ("final", b, 0), ("final", b, 1))
+        low = pl.ds(0, 64)
         for h in range(2):
-            yfinal[q, h] = yfinal[q, h] + ydirect[q, h] + share(y, h, q)[...]
-        znew[q, 0] = send(yfinal.at[q, 1 - zh], zrecv.at[q, 0], dev_z)
-
-    def z_last(q):
-        znew[q, 0].wait_recv()
-        res[pl.ds(q * 8, 8), :] = zrecv[q, 0] + yfinal[q, zh]
-
-    def z_first(q):
-        for i, t in enumerate((across, up, down, y)):
-            znew[q, i].wait_recv()
-            zsum[q, i] = zrecv[q, i] + share(t, zh, q)[...]
-            if i == 0:
-                relay[q, 0] = send(
-                    zsum.at[q, 0, :, pl.ds(0, 2048)], yrelay.at[q, 0, :, pl.ds(0, 2048)], dev_up
-                )
-                relay[q, 1] = send(
-                    zsum.at[q, 0, :, pl.ds(2048, 2048)], yrelay.at[q, 1, :, pl.ds(0, 2048)], dev_down
-                )
-            if i == 1:
-                direct[q, 0] = send(
-                    zsum.at[q, 1, :, pl.ds(2048, 2048)], ydirect.at[q, 1, :, pl.ds(0, 2048)], dev_up
-                )
-            if i == 2:
-                direct[q, 1] = send(
-                    zsum.at[q, 2, :, pl.ds(0, 2048)], ydirect.at[q, 0, :, pl.ds(0, 2048)], dev_down
-                )
-
-    def y_relay_last(q):
-        relay[q, 0].wait_recv()
-        yrelay[q, 0, :, :2048] = yrelay[q, 0, :, :2048] + zsum[q, 1, :, half[0]]
-        final[q, 0] = send(
-            yrelay.at[q, 0, :, pl.ds(0, 2048)], yfinal.at[q, 0, :, pl.ds(0, 2048)], dev_up
-        )
-        relay[q, 1].wait_recv()
-        yrelay[q, 1, :, :2048] = yrelay[q, 1, :, :2048] + zsum[q, 2, :, half[1]]
-        final[q, 1] = send(
-            yrelay.at[q, 1, :, pl.ds(0, 2048)], yfinal.at[q, 1, :, pl.ds(0, 2048)], dev_down
-        )
-
-    def y_last(q):
-        for h in range(2):
-            direct[q, h].wait_recv()
-            final[q, h].wait_recv()
-        for h in range(2):
-            res[pl.ds(q * 8, 8), half[h]] = (
-                zsum[q, 3, :, half[h]] + yfinal[q, h, :, :2048] + ydirect[q, h, :, :2048]
-            )
-
-    y_relay_first(yf[0])
-    idle()
-    y_relay_first(yf[1])
-    y_finish_first(yf[0])
-    z_first(zf[0])
-    y_relay_last(zf[0])
-    y_finish_first(yf[1])
-    z_first(zf[1])
-    y_relay_last(zf[1])
-    y_last(zf[0])
-    z_last(yf[0])
-    z_last(yf[1])
-    y_last(zf[1])
-    return sends
+            rows = pl.ds(h * 64, 64)
+            new = self.yfinal[b, h, low] + self.ydirect[b, h, low]
+            self.total[b, rows] = self.zsum[b, 3, rows] + new
 
 
 def kernel(
     density, weight, bins_in, mats_in, out_real, out_imag, out_spec,
-    recvc, specs, ctw, rtw, mine, res, mats, yrelay, ydirect, yfinal, zrecv, zsum,
-    ubuf, msgb, recvb, msgc, power, acc, spec, raw, near, far, farin, extra,
+    recvc, specs, ctw, rtw, mine, spread, total, mats, yrelay, ydirect, yfinal, zrecv, zsum,
+    ubuf, recvb, msgc, power, acc, spec, raw, near, far, farin, extra,
     lsem, msem, bsem, fsem, ssem, rsem, asem,
 ):
     me = my_index()
@@ -531,23 +515,84 @@
 
     lax.fori_loop(1, DEVICES, greet, 0)
     w = weight[0]
-    for i in range(8):
-        loads[i].wait()
-        rows = pl.ds(i * 32, 32)
-        mine[rows, :] = mine[rows, :] * w
+    mload.wait()
+    read_twiddles(mats, ctw, rtw)
+    row, plane = me // 8, lax.rem(me, 8)
+    red = Reduction(spread, total, yrelay, ydirect, yfinal, zrecv, zsum, ssem, rsem)
+
+    def transform(b):
+        loads[b].wait()
+        row_forward(b, w, mine, mats, rtw, ubuf, spread)
+
+    def to_columns(b):
+        at = pl.ds(pl.multiple_of((row * 8 + b) * 8, 8), 8)
+
+        def step(i, _):
+            to = lax.rem(row + i * 5, 16)
+            pltpu.make_async_remote_copy(
+                src_ref=total.at[b, pl.ds(pl.multiple_of(to * 8, 8), 8)],
+                dst_ref=recvb.at[at],
+                send_sem=asem.at[0],
+                recv_sem=asem.at[1],
+                device_id=to * 8 + plane,
+                device_id_type=LOGICAL,
+            ).start()
+            return 0
+
+        lax.fori_loop(1, 16, step, 0)
+        recvb[at, :] = total[b, pl.ds(pl.multiple_of(row * 8, 8), 8), :]
+
+    transform(5)
     pl.semaphore_wait(barrier, DEVICES - 1)
-
-    def idle():
-        mload.wait()
-        read_twiddles(mats, ctw, rtw)
-        bload.wait()
-        arrange_bins(me, raw, near, far)
-
-    sends = reduce_planes(
-        idle, mine, res, (0, 1), (2, 3), yrelay, ydirect, yfinal, zrecv, zsum, ssem, rsem
-    )
-    row_forward(res, mats, rtw, ubuf, msgb)
-    send_all(me, msgb, recvb, asem.at[0], asem.at[1], 8)
+    red.z_start(5)
+    transform(0)
+    red.y_start(0)
+    transform(6)
+    red.z_start(6)
+    transform(1)
+    red.y_start(1)
+    red.y_relay(0)
+    transform(7)
+    red.z_start(7)
+    transform(2)
+    red.y_start(2)
+    red.y_relay(1)
+    transform(3)
+    transform(4)
+    red.z_then_y(5)
+    red.y_start(3)
+    red.y_relay(2)
+    red.y_finish(0)
+    red.y_relay_half(5)
+    bload.wait()
+    arrange_bins(me, raw, near, far)
+    red.y_start(4)
+    red.y_relay(3)
+    red.y_finish(1)
+    red.z_then_y(6)
+    red.y_relay(4)
+    red.y_relay_half(6)
+    red.y_finish(2)
+    red.y_last(5)
+    to_columns(5)
+    red.z_last(0)
+    to_columns(0)
+    red.y_finish(3)
+    red.z_then_y(7)
+    red.z_last(1)
+    to_columns(1)
+    red.y_relay_half(7)
+    red.y_finish(4)
+    red.y_last(6)
+    to_columns(6)
+    red.z_last(2)
+    to_columns(2)
+    red.z_last(3)
+    to_columns(3)
+    red.y_last(7)
+    to_columns(7)
+    red.z_last(4)
+    to_columns(4)
     mirror = pltpu.make_async_remote_copy(
         src_ref=far,
         dst_ref=farin,
@@ -570,9 +615,12 @@
     def _():
         zeroth.start()
 
-    wait_all(recvb, asem.at[1], 8)
-    column_part(me, recvb, mats, ctw, power, msgc)
-    send_all(me, msgc, recvc, asem.at[2], asem.at[3], 16)
+    wait_all(recvb, asem.at[1], 8, 120)
+
+    def to_rows(ac):
+        send_all(me, ac, msgc, recvc, asem.at[2 + ac], asem.at[6 + ac])
+
+    column_part(me, recvb, mats, ctw, power, msgc, to_rows)
     mirror.wait_recv()
 
     @pl.when(me >= 64)
@@ -597,17 +645,20 @@
 
     lax.fori_loop(1, DEVICES, share_spec, 0)
     specs[me] = spec[0]
-    wait_all(recvc, asem.at[3], 16)
-    row_inverse(recvc, mats, rtw, ubuf, (out_real, out_imag))
+    wait_all(recvc, asem.at[6], 8)
+    row_inverse(0, recvc, mats, rtw, ubuf, out_real)
+    wait_all(recvc, asem.at[7], 8)
+    row_inverse(1, recvc, mats, rtw, ubuf, out_imag)
     wait_all(specs, asem.at[5], 1)
-    total = specs[0]
+    power_sum = specs[0]
     for i in range(1, DEVICES):
-        total = total + specs[i]
-    out_spec[...] = total[:, :NBINS]
-    wait_all(msgb, asem.at[0], 8)
-    wait_all(msgc, asem.at[2], 16)
+        power_sum = power_sum + specs[i]
+    out_spec[...] = power_sum[:, :NBINS]
+    wait_all(recvb, asem.at[0], 8, 120)
+    wait_all(msgc, asem.at[2], 8)
+    wait_all(msgc, asem.at[3], 8)
     wait_all(specs, asem.at[4], 1)
-    for copy in sends:
+    for copy in red.sends:
         copy.wait_send()
     mirror.wait_send()
 
@@ -630,7 +681,7 @@
     hbm = pl.BlockSpec(memory_space=pltpu.HBM)
     smem = pl.BlockSpec(memory_space=pltpu.SMEM)
     dma = pltpu.SemaphoreType.DMA
-    share = (8, 4096)
+    share = (128, 128)
     params = partial(pltpu.CompilerParams, vmem_limit_bytes=55050240)
     shapes = (
         jax.ShapeDtypeStruct((32, N), F32),
@@ -649,15 +700,15 @@
             pltpu.VMEM((2, 128, 128), F32),
             pltpu.VMEM((2, 16, 128), F32),
             pltpu.VMEM((256, N), F32),
-            pltpu.VMEM((32, N), F32),
+            pltpu.VMEM((8 * 1024, 128), F32),
+            pltpu.VMEM((8,) + share, F32),
             pltpu.VMEM((7, 2, 256, 256), BF16),
-            pltpu.VMEM((4, 2) + share, F32),
-            pltpu.VMEM((4, 2) + share, F32),
-            pltpu.VMEM((4, 2) + share, F32),
-            pltpu.VMEM((4, 4) + share, F32),
-            pltpu.VMEM((4, 4) + share, F32),
+            pltpu.VMEM((8, 2) + share, F32),
+            pltpu.VMEM((8, 2) + share, F32),
+            pltpu.VMEM((8, 2) + share, F32),
+            pltpu.VMEM((8, 4) + share, F32),
+            pltpu.VMEM((8, 4) + share, F32),
             pltpu.VMEM((2, 512, 128), F32),
-            pltpu.VMEM((DEVICES * 8, 128), F32),
             pltpu.VMEM((DEVICES * 8, 128), F32),
             pltpu.VMEM((DEVICES * 16, 128), F32),
             pltpu.VMEM((5, 128, 128), F32),
@@ -672,9 +723,9 @@
             dma,
             dma,
             dma((4,)),
-            dma((40,)),
-            dma((40,)),
-            dma((6,)),
+            dma((80,)),
+            dma((80,)),
+            dma((8,)),
         ],
         compiler_params=params(collective_id=0, has_side_effects=True),
     )(density, lens_weight, spectrum_bin.T, mats)

time: 76.7 us -> 75.5 us (0.984)
  Pallas kernels: 75.3 us -> 74 us
    pallas_call x1, Pallas kernels: 74.3 us -> 73 us  [on_device(): pl.pallas_call(kernel, name='shear', out_shape=shapes, in_specs=[hbm, sme...]
where the time goes in v2:
time: 75.5 us; the launch traced here: 75.4 us
  Pallas kernels  74 us (98%)
  between operations  1.44 us (2%)
    pallas_call x1, Pallas kernels, on_device(): pl.pallas_call(kernel, name='shear', out_shape=shapes, in_specs=[hbm, sme...  73 us

profile of v2, /device:TPU:1, one launch (start us, length us, event | category | flops | bytes accessed | tf_op | source)
XLA Modules:
  0.0 75.4 jit_solution(16842613869489629106)
XLA Ops:
  1.3 73.0 %shear.1 = (f32[32,4096]{1,0:T(8,128)S(1)}, f32[32,4096]{1,0:T(8,128)S(1)}, f32[1,64]{1,0:T(1,128)S(1)}) custom-call(f32[1,256,4096]{2,1,0:T(8,128)} %density.1, f32[1]{0:T(128)S(6)} %copy.7.weight, s32[32,4096]{1,0:T(8,128)} %bitcast.2, bf16[7,2,256,256]{3,2,1,0:T(8,128)(2,1)} %constant.2.clone.mats_in), custom_call_target="tpu_custom_call" | custom-call | tf_op jit(solution)/shard_map/shear/pallas_call | solution.py:691
  74.3 1.0 %finish.1 = (f32[32,4096]{1,0:T(8,128)}, f32[32,4096]{1,0:T(8,128)}, f32[1,64]{1,0:T(1,128)}) custom-call(f32[32,4096]{1,0:T(8,128)S(1)} %get-tuple-element.9.refs_0_, f32[32,4096]{1,0:T(8,128)S(1)} %get-tuple-element.10.refs_1_, f32[1,64]{1,0:T(1,128)S(1)} %get-tuple-element.11.refs_2_), custom_call_target="tpu_custom_call" | custom-call | tf_op jit(solution)/shard_map/finish/pallas_call | solution.py:732

commit v3 on v2

--- a/solution.py
+++ b/solution.py
@@ -543,9 +543,9 @@
         recvb[at, :] = total[b, pl.ds(pl.multiple_of(row * 8, 8), 8), :]
 
     transform(5)
+    transform(0)
     pl.semaphore_wait(barrier, DEVICES - 1)
     red.z_start(5)
-    transform(0)
     red.y_start(0)
     transform(6)
     red.z_start(6)

time: 75.5 us -> 74.8 us (level)
  Pallas kernels: 74 us -> 73.2 us
where the time goes in v3:
time: 74.8 us; the launch traced here: 74.7 us
  Pallas kernels  73.2 us (98%)
  between operations  1.44 us (2%)
    pallas_call x1, Pallas kernels, on_device(): pl.pallas_call(kernel, name='shear', out_shape=shapes, in_specs=[hbm, sme...  72.2 us

profile of v3, /device:TPU:1, one launch (start us, length us, event | category | flops | bytes accessed | tf_op | source)
XLA Modules:
  0.0 74.7 jit_solution(14707774300820967246)
XLA Ops:
  1.3 72.2 %shear.1 = (f32[32,4096]{1,0:T(8,128)S(1)}, f32[32,4096]{1,0:T(8,128)S(1)}, f32[1,64]{1,0:T(1,128)S(1)}) custom-call(f32[1,256,4096]{2,1,0:T(8,128)} %density.1, f32[1]{0:T(128)S(6)} %copy.7.weight, s32[32,4096]{1,0:T(8,128)} %bitcast.2, bf16[7,2,256,256]{3,2,1,0:T(8,128)(2,1)} %constant.2.clone.mats_in), custom_call_target="tpu_custom_call" | custom-call | tf_op jit(solution)/shard_map/shear/pallas_call | solution.py:691
  73.5 1.0 %finish.1 = (f32[32,4096]{1,0:T(8,128)}, f32[32,4096]{1,0:T(8,128)}, f32[1,64]{1,0:T(1,128)}) custom-call(f32[32,4096]{1,0:T(8,128)S(1)} %get-tuple-element.9.refs_0_, f32[32,4096]{1,0:T(8,128)S(1)} %get-tuple-element.10.refs_1_, f32[1,64]{1,0:T(1,128)S(1)} %get-tuple-element.11.refs_2_), custom_call_target="tpu_custom_call" | custom-call | tf_op jit(solution)/shard_map/finish/pallas_call | solution.py:732

commit v4 on v3

--- a/solution.py
+++ b/solution.py
@@ -495,15 +495,15 @@
 ):
     me = my_index()
     barrier = pltpu.get_barrier_semaphore()
-    loads = []
-    for i in range(8):
+    mload = pltpu.make_async_copy(mats_in, mats, msem)
+    mload.start()
+    loads = {}
+    for i in (5, 0, 6, 1, 7, 2, 3, 4):
         copy = pltpu.make_async_copy(
             density.at[0, pl.ds(i * 32, 32)], mine.at[pl.ds(i * 32, 32)], lsem.at[i]
         )
         copy.start()
-        loads.append(copy)
-    mload = pltpu.make_async_copy(mats_in, mats, msem)
-    mload.start()
+        loads[i] = copy
     bload = pltpu.make_async_copy(bins_in, raw, bsem)
     bload.start()
 

time: 74.8 us -> 74.7 us (level)
  no operation moved by 1% of the time
where the time goes in v4:
time: 74.7 us; the launch traced here: 74.6 us
  Pallas kernels  73.2 us (98%)
  between operations  1.44 us (2%)
    pallas_call x1, Pallas kernels, on_device(): pl.pallas_call(kernel, name='shear', out_shape=shapes, in_specs=[hbm, sme...  72.2 us

profile of v4, /device:TPU:1, one launch (start us, length us, event | category | flops | bytes accessed | tf_op | source)
XLA Modules:
  0.0 74.6 jit_solution(13889209949772482134)
XLA Ops:
  1.3 72.2 %shear.1 = (f32[32,4096]{1,0:T(8,128)S(1)}, f32[32,4096]{1,0:T(8,128)S(1)}, f32[1,64]{1,0:T(1,128)S(1)}) custom-call(f32[1,256,4096]{2,1,0:T(8,128)} %density.1, f32[1]{0:T(128)S(6)} %copy.7.weight, s32[32,4096]{1,0:T(8,128)} %bitcast.2, bf16[7,2,256,256]{3,2,1,0:T(8,128)(2,1)} %constant.2.clone.mats_in), custom_call_target="tpu_custom_call" | custom-call | tf_op jit(solution)/shard_map/shear/pallas_call | solution.py:691
  73.5 1.0 %finish.1 = (f32[32,4096]{1,0:T(8,128)}, f32[32,4096]{1,0:T(8,128)}, f32[1,64]{1,0:T(1,128)}) custom-call(f32[32,4096]{1,0:T(8,128)S(1)} %get-tuple-element.9.refs_0_, f32[32,4096]{1,0:T(8,128)S(1)} %get-tuple-element.10.refs_1_, f32[1,64]{1,0:T(1,128)S(1)} %get-tuple-element.11.refs_2_), custom_call_target="tpu_custom_call" | custom-call | tf_op jit(solution)/shard_map/finish/pallas_call | solution.py:732
